TPU v7x, 256 devices: a whole 4x4x8 slice. The times are simulated.
256 devices in a mesh: section: 4 (over y_hi, core), replica: 64 (over x, z, y_lo).
Axes of the slice: x: 4, y: 4 (y_hi: 2, y_lo: 2; y = y_hi * 2 + y_lo), z: 8, core: 2. Of those that a mesh axis runs over, the one named last changes fastest.
Arguments:
- tokens: bfloat16 [64, 128, 2048], P('replica', 'section'), may hold values from -6 to 6
- gate_weight: bfloat16 [4, 64, 2048, 384], P('section', 'replica'), may hold values from -0.125 to 0.125
- up_weight: bfloat16 [4, 64, 2048, 384], P('section', 'replica'), may hold values from -0.125 to 0.125
- slow_down: float32 [4, 64, 384, 2048], P('section', 'replica'), may hold values from -0.3125 to 0.3125
- prev_outer: bfloat16 [4, 64, 384, 2048], P('section', 'replica'), may hold values from -0.29882812 to 0.29882812
- route: int32 [3, 1, 64], replicated, may hold values from 0 to 63, each once within a row
- partner: int32 [64], replicated, may hold values from 0 to 63, as said below
Outputs:
- new_slow: float32 [4, 64, 384, 2048], P('section', 'replica')
- new_outer: bfloat16 [4, 64, 384, 2048], P('section', 'replica')
Inputs may be any that keep to these rules, and one draw needn't show every extreme that they name: route[s, m] is a permutation of the replicas: replica r at section s hands micro-batch m to replica route[s, m, r] at section s + 1. partner pairs the replicas: partner[partner[r]] = r and partner[r] != r.
All inputs are finite; a program needn't handle non-finite values.
Results may differ from a plain program's by a relative error of at most 0.017.
Values may be sent and summed in bfloat16 or wider, within the bound.
A program may use at most 128 MiB of HBM per device.

v0:
```python
import jax
import jax.numpy as jnp
from jax import lax
from jax.sharding import Mesh
from jax.sharding import PartitionSpec as P

MT = 128
MB = 1
SECTION = ("section_0", "section_1")


EPSILON = 1e-05
OUTER_RATE = 0.7
MOMENTUM = 0.9


def for_sending(shard):
    return jax.tree.map(lambda a: a.astype(jnp.bfloat16) if a.dtype == jnp.float32 else a, shard)


def in_order(tiles, dim):
    lengths = list(tiles.shape[1:])
    lengths[dim] *= tiles.shape[0]
    return jnp.moveaxis(tiles, 0, dim).reshape(lengths)


def gather_in_order(shard, axes, order):
    tiles = shard[None]
    for k in order:
        tiles = lax.all_gather(tiles, axes[k], axis=0, tiled=True)
    current = [lax.axis_size(axes[k]) for k in reversed(order)]
    tiles = tiles.reshape(*current, *shard.shape)
    turned = sorted(range(len(order)), key=lambda place: order[len(order) - 1 - place])
    return tiles.transpose(*turned, *range(len(order), tiles.ndim)).reshape(-1, *shard.shape)


def gather_axes(shard, axes, order, dim):
    return in_order(gather_in_order(shard, axes, order), dim)


def passed_along(shard, axis, by):
    length = lax.axis_size(axis)
    pairs = [(i, i + by) for i in range(length) if 0 <= i + by < length]
    return lax.ppermute(shard, axis, pairs)


def section_forward(inputs, gate_w, up_w, down_w):
    widened = inputs.astype(jnp.float32)
    inv_rms = lax.rsqrt(jnp.mean(widened * widened, axis=-1, keepdims=True) + EPSILON)
    normed = (widened * inv_rms).astype(jnp.bfloat16)
    gate_act = jnp.dot(normed, gate_w, preferred_element_type=jnp.float32)
    up_act = jnp.dot(normed, up_w, preferred_element_type=jnp.float32)
    hidden = (jax.nn.silu(gate_act) * up_act).astype(jnp.bfloat16)
    output = (widened + jnp.dot(hidden, down_w, preferred_element_type=jnp.float32)).astype(
        jnp.bfloat16
    )
    return (output, gate_act, up_act, hidden)


def section_backward(inputs, gate_act, up_act, hidden, upstream, gate_w, up_w, down_w):
    contract_rows = (((0,), (0,)), ((), ()))
    contract_cols = (((1,), (1,)), ((), ()))
    grad_part = lax.dot_general(hidden, upstream, contract_rows, preferred_element_type=jnp.float32)
    hidden_grad = lax.dot_general(
        upstream, down_w, contract_cols, preferred_element_type=jnp.float32
    )
    sigmoid_gate = jax.nn.sigmoid(gate_act)
    gate_grad = (
        hidden_grad * up_act * sigmoid_gate * (1.0 + gate_act * (1.0 - sigmoid_gate))
    ).astype(jnp.bfloat16)
    up_grad = (hidden_grad * gate_act * sigmoid_gate).astype(jnp.bfloat16)
    normed_grad = lax.dot_general(
        gate_grad, gate_w, contract_cols, preferred_element_type=jnp.float32
    )
    normed_grad = normed_grad + lax.dot_general(
        up_grad, up_w, contract_cols, preferred_element_type=jnp.float32
    )
    widened = inputs.astype(jnp.float32)
    inv_rms = lax.rsqrt(jnp.mean(widened * widened, axis=-1, keepdims=True) + EPSILON)
    input_grad = upstream.astype(jnp.float32) + inv_rms * normed_grad
    input_grad = input_grad - widened * inv_rms**3 * jnp.mean(
        normed_grad * widened, axis=-1, keepdims=True
    )
    return (grad_part, input_grad.astype(jnp.bfloat16))


def permute_matrix(targets, replica_count):
    return (targets[None, :] == jnp.arange(replica_count, dtype=jnp.int32)[:, None]).astype(
        jnp.bfloat16
    )


def reorder(received, matrix):
    flat_rows = received.reshape(received.shape[0], -1)
    placed = jnp.dot(matrix, flat_rows, preferred_element_type=jnp.float32).astype(jnp.bfloat16)
    return placed.reshape(received.shape)


def route_block(act_block, matrix):
    return lax.all_to_all(
        reorder(
            lax.all_to_all(act_block[None], "replica", split_axis=1, concat_axis=0, tiled=True),
            matrix,
        ),
        "replica",
        split_axis=0,
        concat_axis=1,
        tiled=True,
    )[0]


def partner_copy(slow_weight, prior_outer, partner):
    received = (
        lax.all_to_all(
            slow_weight[None].astype(jnp.bfloat16),
            "replica",
            split_axis=1,
            concat_axis=0,
            tiled=True,
        ).astype(jnp.float32),
        lax.all_to_all(prior_outer[None], "replica", split_axis=1, concat_axis=0, tiled=True),
    )
    mates = lax.all_to_all(
        for_sending(tuple((jnp.take(member, partner, axis=0) for member in received))),
        "replica",
        split_axis=0,
        concat_axis=1,
        tiled=True,
    )
    return (mates[0][0], mates[1][0])


def store_slot(buffer, slot_index, is_live, new_value):
    previous = buffer[slot_index]
    return buffer.at[slot_index].set(jnp.where(is_live, new_value, previous))


def local(tokens, gate_weight, up_weight, slow_down, prev_outer, route, partner):
    section_count = lax.axis_size(SECTION)
    replica_count = lax.axis_size("replica")
    section_id = lax.axis_index(SECTION)
    gate_w = gate_weight[0, 0]
    up_w = up_weight[0, 0]
    slow_weight = slow_down[0, 0]
    prior_outer = prev_outer[0, 0]
    down_w = slow_weight.astype(jnp.bfloat16)
    feature_count = gate_w.shape[0]
    hidden_units = gate_w.shape[1]
    gathered = gather_axes(tokens[0], ("section_0", "section_1"), (0, 1), 0).reshape(
        MB, MT, feature_count
    )
    turn_count = MB + section_count - 1
    saved_in = jnp.zeros((MB, MT, feature_count), jnp.bfloat16)
    saved_out = jnp.zeros((MB, MT, feature_count), jnp.bfloat16)
    saved_gate = jnp.zeros((MB, MT, hidden_units), jnp.float32)
    saved_up = jnp.zeros((MB, MT, hidden_units), jnp.float32)
    saved_hidden = jnp.zeros((MB, MT, hidden_units), jnp.bfloat16)
    arriving = jnp.zeros((MT, feature_count), jnp.bfloat16)
    for turn_index in range(turn_count):
        micro_batch = turn_index - section_id
        is_live = (micro_batch >= 0) & (micro_batch < MB)
        slot_index = jnp.clip(micro_batch, 0, MB - 1)
        fresh_rows = gathered[min(turn_index, MB - 1)]
        inputs = jnp.where(section_id == 0, fresh_rows, arriving)
        output, gate_act, up_act, hidden = section_forward(inputs, gate_w, up_w, down_w)
        saved_in = store_slot(saved_in, slot_index, is_live, inputs)
        saved_out = store_slot(saved_out, slot_index, is_live, output)
        saved_gate = store_slot(saved_gate, slot_index, is_live, gate_act)
        saved_up = store_slot(saved_up, slot_index, is_live, up_act)
        saved_hidden = store_slot(saved_hidden, slot_index, is_live, hidden)
        if turn_index < turn_count - 1:
            boundary = jnp.minimum(section_id, section_count - 2)
            matrix = permute_matrix(route[boundary, slot_index], replica_count)
            arriving = passed_along(route_block(output, matrix), SECTION, 1)
    weight_grad = jnp.zeros((hidden_units, feature_count), jnp.float32)
    arriving = jnp.zeros((MT, feature_count), jnp.bfloat16)
    for turn_index in range(turn_count):
        micro_batch = turn_index - (section_count - 1 - section_id)
        is_live = (micro_batch >= 0) & (micro_batch < MB)
        slot_index = jnp.clip(micro_batch, 0, MB - 1)
        loss_grad = (saved_out[slot_index].astype(jnp.float32) / float(MB * MT)).astype(
            jnp.bfloat16
        )
        upstream = jnp.where(section_id == section_count - 1, loss_grad, arriving)
        grad_part, input_grad = section_backward(
            saved_in[slot_index],
            saved_gate[slot_index],
            saved_up[slot_index],
            saved_hidden[slot_index],
            upstream,
            gate_w,
            up_w,
            down_w,
        )
        weight_grad = weight_grad + jnp.where(is_live, grad_part, 0.0)
        if turn_index < turn_count - 1:
            boundary = jnp.maximum(section_id - 1, 0)
            matrix = permute_matrix(route[boundary, slot_index], replica_count).T
            arriving = passed_along(route_block(input_grad, matrix), SECTION, -1)
    mate_slow, mate_prior = partner_copy(slow_weight, prior_outer, partner)
    average_slow = 0.5 * (slow_weight + mate_slow)
    average_prev = 0.5 * (prior_outer.astype(jnp.float32) + mate_prior.astype(jnp.float32))
    velocity = MOMENTUM * average_prev + weight_grad
    new_slow = average_slow - OUTER_RATE * (weight_grad + MOMENTUM * velocity)
    return (new_slow[None, None], velocity.astype(jnp.bfloat16)[None, None])


def solution(mesh):
    torus = Mesh(
        mesh.devices.reshape(2, 2, mesh.shape["replica"]), ("section_0", "section_1", "replica")
    )
    return jax.shard_map(
        local,
        mesh=torus,
        in_specs=(
            P("replica", SECTION, None),
            P(SECTION, "replica", None, None),
            P(SECTION, "replica", None, None),
            P(SECTION, "replica", None, None),
            P(SECTION, "replica", None, None),
            P(),
            P(),
        ),
        out_specs=(P(SECTION, "replica", None, None), P(SECTION, "replica", None, None)),
        check_vma=False,
    )
```

profile of v0, /device:TPU:1, one launch (start us, length us, event | category | flops | bytes accessed | tf_op | source)
XLA Modules:
  0.0 743.4 jit_solution(11176813769003654150)
XLA Ops:
  0.6 7.2 all_gather.6
  7.8 5.3 all_gather.7
  14.1 4.6 bitcast_convert_fusion
  23.9 5.5 reduce.83
  31.5 11.7 %all-to-all-start.2 = ((bf16[64,2,2048]{2,1,0:T(2,128)(2,1)}), bf16[64,2,2048]{2,1,0:T(2,128)(2,1)}, u32[]{:S(2)}, u32[]{:S(2)}) async-start(bf16[64,2,2048]{2,1,0:T(2,128)(2,1)} %reshape.880), calls=%async_computation.2 | async-start | bytes 1048576 | tf_op jit(solution)/shard_map/all_to_all | solution.py:102
  43.3 15.8 %all-to-all-done.2 = bf16[64,2,2048]{2,1,0:T(2,128)(2,1)} async-done(((bf16[64,2,2048]{2,1,0:T(2,128)(2,1)}), bf16[64,2,2048]{2,1,0:T(2,128)(2,1)}, u32[]{:S(2)}, u32[]{:S(2)}) %all-to-all-start.2) | async-done | bytes 524320 | tf_op jit(solution)/shard_map/all_to_all | solution.py:102
  59.1 4.4 reshape.881
  63.5 5.0 bitcast_reduce_fusion.6
  74.9 22.9 %all_to_all.67 = bf16[64,2,2048]{2,1,0:T(2,128)(2,1)} all-to-all(bf16[64,2,2048]{2,1,0:T(2,128)(2,1)} %reshape.837), channel_id=1, replica_groups=mesh['section_0'=2,'section_1'=2,'replica'=64] {'replica'}, dimensions={0} | all-to-all | bytes 1048576 | tf_op jit(solution)/shard_map/all_to_all | solution.py:100
  99.9 7.5 %collective-permute-start = (bf16[128,2048]{1,0:T(8,128)(2,1)}, bf16[128,2048]{1,0:T(8,128)(2,1)S(1)}, u32[]{:S(2)}, u32[]{:S(2)}) collective-permute-start(bf16[128,2048]{1,0:T(8,128)(2,1)} %squeeze.23), channel_id=1, source_target_pairs={{0,64},{64,128},{128,192},{1,65},{65,129},{129,193},{2,66},{66,130... | collective-permute-start | bytes 1572872 | tf_op jit(solution)/shard_map/ppermute | solution.py:44
  107.4 6.4 collective-permute-done
  120.2 5.5 reduce.84
  127.9 30.8 %all_to_all.68 = bf16[64,2,2048]{2,1,0:T(2,128)(2,1)} all-to-all(bf16[64,2,2048]{2,1,0:T(2,128)(2,1)} %reshape.882), channel_id=1, replica_groups=mesh['section_0'=2,'section_1'=2,'replica'=64] {'replica'}, dimensions={0} | all-to-all | bytes 1048576 | tf_op jit(solution)/shard_map/all_to_all | solution.py:102
  158.6 4.4 reshape.883
  163.1 5.0 bitcast_reduce_fusion.5
  174.5 18.6 %all_to_all.69 = bf16[64,2,2048]{2,1,0:T(2,128)(2,1)} all-to-all(bf16[64,2,2048]{2,1,0:T(2,128)(2,1)} %reshape.839), channel_id=1, replica_groups=mesh['section_0'=2,'section_1'=2,'replica'=64] {'replica'}, dimensions={0} | all-to-all | bytes 1048576 | tf_op jit(solution)/shard_map/all_to_all | solution.py:100
  195.1 8.4 %collective-permute-start.1 = (bf16[128,2048]{1,0:T(8,128)(2,1)}, bf16[128,2048]{1,0:T(8,128)(2,1)S(1)}, u32[]{:S(2)}, u32[]{:S(2)}) collective-permute-start(bf16[128,2048]{1,0:T(8,128)(2,1)} %squeeze.24), channel_id=1, source_target_pairs={{0,64},{64,128},{128,192},{1,65},{65,129},{129,193},{2,66},{66,130... | collective-permute-start | bytes 1572872 | tf_op jit(solution)/shard_map/ppermute | solution.py:44
  203.5 6.4 collective-permute-done.1
  216.4 5.5 reduce.85
  224.0 17.8 %all_to_all.70 = bf16[64,2,2048]{2,1,0:T(2,128)(2,1)} all-to-all(bf16[64,2,2048]{2,1,0:T(2,128)(2,1)} %reshape.884), channel_id=1, replica_groups=mesh['section_0'=2,'section_1'=2,'replica'=64] {'replica'}, dimensions={0} | all-to-all | bytes 1048576 | tf_op jit(solution)/shard_map/all_to_all | solution.py:102
  241.8 4.4 reshape.885
  246.2 5.0 bitcast_reduce_fusion.4
  257.6 18.2 %all_to_all.71 = bf16[64,2,2048]{2,1,0:T(2,128)(2,1)} all-to-all(bf16[64,2,2048]{2,1,0:T(2,128)(2,1)} %reshape.841), channel_id=1, replica_groups=mesh['section_0'=2,'section_1'=2,'replica'=64] {'replica'}, dimensions={0} | all-to-all | bytes 1048576 | tf_op jit(solution)/shard_map/all_to_all | solution.py:100
  277.8 8.9 %collective-permute-start.2 = (bf16[128,2048]{1,0:T(8,128)(2,1)}, bf16[128,2048]{1,0:T(8,128)(2,1)}, u32[]{:S(2)}, u32[]{:S(2)}) collective-permute-start(bf16[128,2048]{1,0:T(8,128)(2,1)} %squeeze.25), channel_id=1, source_target_pairs={{0,64},{64,128},{128,192},{1,65},{65,129},{129,193},{2,66},{66,130... | collective-permute-start | bytes 1572872 | tf_op jit(solution)/shard_map/ppermute | solution.py:44
  288.3 4.9 collective-permute-done.2
  294.7 4.0 select_select_fusion.5
  298.7 4.0 select_select_fusion.11
  317.8 5.5 reduce.86
  325.4 5.7 all-to-all-start.8
  331.1 5.5 copy.39
  336.6 12.3 %reduce.81 = bf16[384,2048]{1,0:T(8,128)(2,1)} reduce(bf16[384,1,2048]{2,1,0:T(2,128)(2,1)} %bitcast.177, bf16[]{:T(256)} %broadcast.524), dimensions={1}, to_apply=%bitcast.168.reduce_sub_computation | reduce | bytes 3145730
  348.9 4.8 reshape.892
  353.7 11.0 %all-to-all-start.14 = ((bf16[64,2,6144]{2,1,0:T(2,128)(2,1)}), bf16[64,2,6144]{2,1,0:T(2,128)(2,1)}, u32[]{:S(2)}, u32[]{:S(2)}) async-start(bf16[64,2,6144]{2,1,0:T(2,128)(2,1)} %reshape.892), calls=%async_computation.14 | async-start | bytes 3145728 | tf_op jit(solution)/shard_map/all_to_all | solution.py:121
  364.7 4.5 reshape.887
  369.2 5.0 bitcast_reduce_fusion.3
  380.6 14.6 %all-to-all-done.14 = bf16[64,2,6144]{2,1,0:T(2,128)(2,1)} async-done(((bf16[64,2,6144]{2,1,0:T(2,128)(2,1)}), bf16[64,2,6144]{2,1,0:T(2,128)(2,1)}, u32[]{:S(2)}, u32[]{:S(2)}) %all-to-all-start.14) | async-done | bytes 1572896 | tf_op jit(solution)/shard_map/all_to_all | solution.py:121
  395.2 6.2 all-to-all-start.9
  401.4 5.5 copy.40
  406.9 12.3 %reduce.82 = bf16[384,2048]{1,0:T(8,128)(2,1)} reduce(bf16[384,1,2048]{2,1,0:T(2,128)(2,1)} %bitcast.176, bf16[]{:T(256)} %broadcast.524), dimensions={1}, to_apply=%bitcast.169.reduce_sub_computation | reduce | bytes 3145730
  419.1 4.7 reshape.878
  423.9 11.0 %all-to-all-start = ((bf16[64,2,6144]{2,1,0:T(2,128)(2,1)}), bf16[64,2,6144]{2,1,0:T(2,128)(2,1)}, u32[]{:S(2)}, u32[]{:S(2)}) async-start(bf16[64,2,6144]{2,1,0:T(2,128)(2,1)} %reshape.878), calls=%async_computation | async-start | bytes 3145728 | tf_op jit(solution)/shard_map/all_to_all | solution.py:114
  439.0 17.8 %collective-permute-done.3 = bf16[128,2048]{1,0:T(8,128)(2,1)S(1)} collective-permute-done((bf16[128,2048]{1,0:T(8,128)(2,1)}, bf16[128,2048]{1,0:T(8,128)(2,1)S(1)}, u32[]{:S(2)}, u32[]{:S(2)}) %collective-permute-start.3) | collective-permute-done | bytes 524320 | tf_op jit(solution)/shard_map/ppermute | solution.py:44
  461.4 5.5 reduce.87
  469.0 11.2 %all-to-all-start.10 = ((bf16[64,2,2048]{2,1,0:T(2,128)(2,1)}), bf16[64,2,2048]{2,1,0:T(2,128)(2,1)}, u32[]{:S(2)}, u32[]{:S(2)}) async-start(bf16[64,2,2048]{2,1,0:T(2,128)(2,1)} %reshape.888), calls=%async_computation.10 | async-start | bytes 1048576 | tf_op jit(solution)/shard_map/all_to_all | solution.py:102
  481.5 10.4 %reshape.893 = bf16[384,1,2048]{2,1,0:T(2,128)(2,1)} reshape(bf16[64,2,6144]{2,1,0:T(2,128)(2,1)} %all-to-all-done.14) | data formatting | bytes 3145728
  491.8 12.2 %bitcast_reduce_fusion = bf16[384,2048]{1,0:T(8,128)(2,1)} fusion(bf16[384,1,2048]{2,1,0:T(2,128)(2,1)} %reshape.893), kind=kLoop, calls=%fused_computation.188 | loop fusion | bytes 3145728 | tf_op jit(solution)/shard_map/all_to_all | solution.py:121
  507.8 10.4 %reshape.879 = bf16[384,1,2048]{2,1,0:T(2,128)(2,1)} reshape(bf16[64,2,6144]{2,1,0:T(2,128)(2,1)} %all-to-all-done) | data formatting | bytes 3145728
  518.1 4.4 reshape.889
  522.6 5.0 bitcast_reduce_fusion.2
  534.0 11.2 %all-to-all-start.11 = ((bf16[64,2,2048]{2,1,0:T(2,128)(2,1)}), bf16[64,2,2048]{2,1,0:T(2,128)(2,1)}, u32[]{:S(2)}, u32[]{:S(2)}) async-start(bf16[64,2,2048]{2,1,0:T(2,128)(2,1)} %reshape.845), calls=%async_computation.11 | async-start | bytes 1048576 | tf_op jit(solution)/shard_map/all_to_all | solution.py:100
  545.3 12.2 %convert_reduce_fusion = bf16[384,2048]{1,0:T(8,128)(2,1)} fusion(bf16[384,1,2048]{2,1,0:T(2,128)(2,1)} %reshape.879), kind=kLoop, calls=%fused_computation.17 | loop fusion | flops 786432 | bytes 3145728 | tf_op jit(solution)/shard_map/convert_element_type | solution.py:120
  568.4 5.9 broadcast_select_fusion
  574.3 11.3 %all-to-all-start.15 = ((bf16[64,6,2048]{2,1,0:T(8,128)(2,1)}), bf16[64,6,2048]{2,1,0:T(8,128)(2,1)}, u32[]{:S(2)}, u32[]{:S(2)}) async-start(bf16[64,6,2048]{2,1,0:T(8,128)(2,1)} %get-tuple-element.259), calls=%async_computation.15 | async-start | bytes 4194304 | tf_op jit(solution)/shard_map/all_to_all | solution.py:123
  589.6 15.1 %collective-permute-done.4 = bf16[128,2048]{1,0:T(8,128)(2,1)S(1)} collective-permute-done((bf16[128,2048]{1,0:T(8,128)(2,1)}, bf16[128,2048]{1,0:T(8,128)(2,1)S(1)}, u32[]{:S(2)}, u32[]{:S(2)}) %collective-permute-start.4) | collective-permute-done | bytes 524320 | tf_op jit(solution)/shard_map/ppermute | solution.py:44
  612.3 16.7 %all-to-all-done.15 = bf16[64,6,2048]{2,1,0:T(8,128)(2,1)} async-done(((bf16[64,6,2048]{2,1,0:T(8,128)(2,1)}), bf16[64,6,2048]{2,1,0:T(8,128)(2,1)}, u32[]{:S(2)}, u32[]{:S(2)}) %all-to-all-start.15) | async-done | bytes 1572896 | tf_op jit(solution)/shard_map/all_to_all | solution.py:123
  629.1 18.0 %all_to_all.72 = bf16[64,2,2048]{2,1,0:T(2,128)(2,1)S(1)} all-to-all(bf16[64,2,2048]{2,1,0:T(2,128)(2,1)S(1)} %reshape.890), channel_id=1, replica_groups=mesh['section_0'=2,'section_1'=2,'replica'=64] {'replica'}, dimensions={0} | all-to-all | bytes 1048576 | tf_op jit(solution)/shard_map/all_to_all | solution.py:102
  647.1 5.8 all-to-all-start.1
  658.2 42.8 %all-to-all-done.1 = bf16[64,6,2048]{2,1,0:T(8,128)(2,1)} async-done(((bf16[64,6,2048]{2,1,0:T(8,128)(2,1)}), bf16[64,6,2048]{2,1,0:T(8,128)(2,1)}, u32[]{:S(2)}, u32[]{:S(2)}) %all-to-all-start.1) | async-done | bytes 1572896 | tf_op jit(solution)/shard_map/all_to_all | solution.py:123
  700.9 5.3 all-to-all-start.13
  706.3 4.0 reshape.849
  710.3 4.0 reshape.851
  716.6 7.7 %all-to-all-done.13 = bf16[64,2,2048]{2,1,0:T(2,128)(2,1)S(1)} async-done(((bf16[64,2,2048]{2,1,0:T(2,128)(2,1)}), bf16[64,2,2048]{2,1,0:T(2,128)(2,1)S(1)}, u32[]{:S(2)}, u32[]{:S(2)}) %all-to-all-start.13) | async-done | bytes 524320 | tf_op jit(solution)/shard_map/all_to_all | solution.py:100
  729.0 8.6 %collective-permute-done.5 = bf16[128,2048]{1,0:T(8,128)(2,1)S(1)} collective-permute-done((bf16[128,2048]{1,0:T(8,128)(2,1)}, bf16[128,2048]{1,0:T(8,128)(2,1)S(1)}, u32[]{:S(2)}, u32[]{:S(2)}) %collective-permute-start.5) | collective-permute-done | bytes 524320 | tf_op jit(solution)/shard_map/ppermute | solution.py:44
  737.6 5.3 fusion.15
  (195 shorter events, 133.7 us)
Async XLA Ops:
  0.6 18.6 %copy-start = (bf16[1,1,2048,384]{3,2,1,0:T(8,128)(2,1)S(1)}, bf16[1,1,2048,384]{3,2,1,0:T(8,128)(2,1)}, u32[]{:S(2)}) copy-start(bf16[1,1,2048,384]{3,2,1,0:T(8,128)(2,1)} %param.49) | copy-start | bytes 4718596
  13.2 0.8 copy-start.15
  14.1 6.3 copy-start.31
  14.1 4.6 copy-start.1
  18.7 1.6 copy-start.2
  20.3 3.0 copy-start.39
  20.8 0.8 copy-start.25
  23.9 19.4 %copy-start.45 = (s32[3,1,64]{2,1,0:T(1,128)S(1)}, s32[3,1,64]{2,1,0:T(1,128)}, u32[]{:S(2)}) copy-start(s32[3,1,64]{2,1,0:T(1,128)} %param.52) | copy-start | bytes 2308
  31.5 27.5 %all-to-all-start.2 = ((bf16[64,2,2048]{2,1,0:T(2,128)(2,1)}), bf16[64,2,2048]{2,1,0:T(2,128)(2,1)}, u32[]{:S(2)}, u32[]{:S(2)}) async-start(bf16[64,2,2048]{2,1,0:T(2,128)(2,1)} %reshape.880), calls=%async_computation.2 | async-start | bytes 1048576 | tf_op jit(solution)/shard_map/all_to_all | solution.py:102
  99.9 14.0 %collective-permute-start = (bf16[128,2048]{1,0:T(8,128)(2,1)}, bf16[128,2048]{1,0:T(8,128)(2,1)S(1)}, u32[]{:S(2)}, u32[]{:S(2)}) collective-permute-start(bf16[128,2048]{1,0:T(8,128)(2,1)} %squeeze.23), channel_id=1, source_target_pairs={{0,64},{64,128},{128,192},{1,65},{65,129},{129,193},{2,66},{66,130... | collective-permute-start | bytes 1572872 | tf_op jit(solution)/shard_map/ppermute | solution.py:44
  115.1 1.7 copy-start.21
  115.7 2.0 copy-start.34
  115.7 1.5 copy-start.3
  116.9 0.8 copy-start.41
  117.7 0.8 copy-start.27
  195.1 14.9 %collective-permute-start.1 = (bf16[128,2048]{1,0:T(8,128)(2,1)}, bf16[128,2048]{1,0:T(8,128)(2,1)S(1)}, u32[]{:S(2)}, u32[]{:S(2)}) collective-permute-start(bf16[128,2048]{1,0:T(8,128)(2,1)} %squeeze.24), channel_id=1, source_target_pairs={{0,64},{64,128},{128,192},{1,65},{65,129},{129,193},{2,66},{66,130... | collective-permute-start | bytes 1572872 | tf_op jit(solution)/shard_map/ppermute | solution.py:44
  211.2 1.7 copy-start.23
  211.7 2.0 copy-start.35
  211.8 1.6 copy-start.4
  212.9 0.8 copy-start.43
  213.8 0.8 copy-start.29
  277.8 15.3 %collective-permute-start.2 = (bf16[128,2048]{1,0:T(8,128)(2,1)}, bf16[128,2048]{1,0:T(8,128)(2,1)}, u32[]{:S(2)}, u32[]{:S(2)}) collective-permute-start(bf16[128,2048]{1,0:T(8,128)(2,1)} %squeeze.25), channel_id=1, source_target_pairs={{0,64},{64,128},{128,192},{1,65},{65,129},{129,193},{2,66},{66,130... | collective-permute-start | bytes 1572872 | tf_op jit(solution)/shard_map/ppermute | solution.py:44
  294.6 4.0 copy-start.40
  294.6 4.0 copy-start.42
  294.7 4.0 copy-start.44
  298.7 4.0 copy-start.5
  298.7 4.0 copy-start.26
  298.7 4.0 copy-start.28
  298.7 4.0 copy-start.30
  302.7 3.5 copy-start.8
  306.2 8.7 %copy-start.10 = (bf16[128,2048]{1,0:T(8,128)(2,1)}, bf16[128,2048]{1,0:T(8,128)(2,1)S(1)}, u32[]{:S(2)}) copy-start(bf16[128,2048]{1,0:T(8,128)(2,1)S(1)} %fusion.13) | copy-start | bytes 1572868
  306.2 1.1 copy-start.36
  306.2 1.2 copy-start.37
  306.2 1.3 copy-start.38
  310.0 1.0 copy-start.22
  310.1 1.2 copy-start.24
  310.1 1.3 copy-start.32
  314.9 0.8 copy-start.12
  325.4 28.3 %all-to-all-start.8 = ((bf16[64,2,2048]{2,1,0:T(2,128)(2,1)}), bf16[64,2,2048]{2,1,0:T(2,128)(2,1)}, u32[]{:S(2)}, u32[]{:S(2)}) async-start(bf16[64,2,2048]{2,1,0:T(2,128)(2,1)} %reshape.886), calls=%async_computation.8 | async-start | bytes 1048576 | tf_op jit(solution)/shard_map/all_to_all | solution.py:102
  353.7 41.5 %all-to-all-start.14 = ((bf16[64,2,6144]{2,1,0:T(2,128)(2,1)}), bf16[64,2,6144]{2,1,0:T(2,128)(2,1)}, u32[]{:S(2)}, u32[]{:S(2)}) async-start(bf16[64,2,6144]{2,1,0:T(2,128)(2,1)} %reshape.892), calls=%async_computation.14 | async-start | bytes 3145728 | tf_op jit(solution)/shard_map/all_to_all | solution.py:121
  395.2 28.7 %all-to-all-start.9 = ((bf16[64,2,2048]{2,1,0:T(2,128)(2,1)}), bf16[64,2,2048]{2,1,0:T(2,128)(2,1)}, u32[]{:S(2)}, u32[]{:S(2)}) async-start(bf16[64,2,2048]{2,1,0:T(2,128)(2,1)} %reshape.843), calls=%async_computation.9 | async-start | bytes 1048576 | tf_op jit(solution)/shard_map/all_to_all | solution.py:100
  423.9 45.1 %all-to-all-start = ((bf16[64,2,6144]{2,1,0:T(2,128)(2,1)}), bf16[64,2,6144]{2,1,0:T(2,128)(2,1)}, u32[]{:S(2)}, u32[]{:S(2)}) async-start(bf16[64,2,6144]{2,1,0:T(2,128)(2,1)} %reshape.878), calls=%async_computation | async-start | bytes 3145728 | tf_op jit(solution)/shard_map/all_to_all | solution.py:114
  436.9 19.9 %copy-start.6 = (bf16[384,2048]{1,0:T(8,128)(2,1)S(1)}, bf16[384,2048]{1,0:T(8,128)(2,1)}, u32[]{:S(2)}) copy-start(bf16[384,2048]{1,0:T(8,128)(2,1)} %copy-done.2) | copy-start | bytes 4718596
  436.9 19.8 %collective-permute-start.3 = (bf16[128,2048]{1,0:T(8,128)(2,1)}, bf16[128,2048]{1,0:T(8,128)(2,1)S(1)}, u32[]{:S(2)}, u32[]{:S(2)}) collective-permute-start(bf16[128,2048]{1,0:T(8,128)(2,1)} %squeeze.27), channel_id=1, source_target_pairs={{64,0},{128,64},{192,128},{65,1},{129,65},{193,129},{66,2},{130,66... | collective-permute-start | bytes 1572872 | tf_op jit(solution)/shard_map/ppermute | solution.py:44
  456.8 2.4 copy-start.17
  457.4 1.0 copy-start.13
  461.4 18.9 %copy-start.46 = (s32[64]{0:T(128)S(1)}, s32[64]{0:T(128)}, u32[]{:S(2)}) copy-start(s32[64]{0:T(128)} %param.53) | copy-start | bytes 772
  469.0 49.1 %all-to-all-start.10 = ((bf16[64,2,2048]{2,1,0:T(2,128)(2,1)}), bf16[64,2,2048]{2,1,0:T(2,128)(2,1)}, u32[]{:S(2)}, u32[]{:S(2)}) async-start(bf16[64,2,2048]{2,1,0:T(2,128)(2,1)} %reshape.888), calls=%async_computation.10 | async-start | bytes 1048576 | tf_op jit(solution)/shard_map/all_to_all | solution.py:102
  534.0 40.2 %all-to-all-start.11 = ((bf16[64,2,2048]{2,1,0:T(2,128)(2,1)}), bf16[64,2,2048]{2,1,0:T(2,128)(2,1)}, u32[]{:S(2)}, u32[]{:S(2)}) async-start(bf16[64,2,2048]{2,1,0:T(2,128)(2,1)} %reshape.845), calls=%async_computation.11 | async-start | bytes 1048576 | tf_op jit(solution)/shard_map/all_to_all | solution.py:100
  574.3 54.8 %all-to-all-start.15 = ((bf16[64,6,2048]{2,1,0:T(8,128)(2,1)}), bf16[64,6,2048]{2,1,0:T(8,128)(2,1)}, u32[]{:S(2)}, u32[]{:S(2)}) async-start(bf16[64,6,2048]{2,1,0:T(8,128)(2,1)} %get-tuple-element.259), calls=%async_computation.15 | async-start | bytes 4194304 | tf_op jit(solution)/shard_map/all_to_all | solution.py:123
  587.6 17.2 %copy-start.7 = (bf16[384,2048]{1,0:T(8,128)(2,1)S(1)}, bf16[384,2048]{1,0:T(8,128)(2,1)}, u32[]{:S(2)}) copy-start(bf16[384,2048]{1,0:T(8,128)(2,1)} %copy-done.2) | copy-start | bytes 4718596
  587.6 17.1 %collective-permute-start.4 = (bf16[128,2048]{1,0:T(8,128)(2,1)}, bf16[128,2048]{1,0:T(8,128)(2,1)S(1)}, u32[]{:S(2)}, u32[]{:S(2)}) collective-permute-start(bf16[128,2048]{1,0:T(8,128)(2,1)} %squeeze.28), channel_id=1, source_target_pairs={{64,0},{128,64},{192,128},{65,1},{129,65},{193,129},{66,2},{130,66... | collective-permute-start | bytes 1572872 | tf_op jit(solution)/shard_map/ppermute | solution.py:44
  604.8 2.4 copy-start.19
  605.4 1.0 copy-start.14
  647.1 53.9 %all-to-all-start.1 = ((bf16[64,6,2048]{2,1,0:T(8,128)(2,1)}), bf16[64,6,2048]{2,1,0:T(8,128)(2,1)}, u32[]{:S(2)}, u32[]{:S(2)}) async-start(bf16[64,6,2048]{2,1,0:T(8,128)(2,1)} %get-tuple-element.260), calls=%async_computation.1 | async-start | bytes 4194304 | tf_op jit(solution)/shard_map/all_to_all | solution.py:123
  700.9 23.3 %all-to-all-start.13 = ((bf16[64,2,2048]{2,1,0:T(2,128)(2,1)}), bf16[64,2,2048]{2,1,0:T(2,128)(2,1)S(1)}, u32[]{:S(2)}, u32[]{:S(2)}) async-start(bf16[64,2,2048]{2,1,0:T(2,128)(2,1)} %reshape.847), calls=%async_computation.13 | async-start | bytes 1048576 | tf_op jit(solution)/shard_map/all_to_all | solution.py:100
  710.3 4.0 copy-start.11
  710.3 4.0 copy-start.33
  714.3 13.4 %copy-start.18 = (bf16[128,2048]{1,0:T(8,128)(2,1)S(1)}, bf16[128,2048]{1,0:T(8,128)(2,1)}, u32[]{:S(2)}) copy-start(bf16[128,2048]{1,0:T(8,128)(2,1)} %copy-done.17) | copy-start | bytes 1572868
  725.3 3.1 copy-start.20
  725.3 12.3 %collective-permute-start.5 = (bf16[128,2048]{1,0:T(8,128)(2,1)}, bf16[128,2048]{1,0:T(8,128)(2,1)S(1)}, u32[]{:S(2)}, u32[]{:S(2)}) collective-permute-start(bf16[128,2048]{1,0:T(8,128)(2,1)} %squeeze.29), channel_id=1, source_target_pairs={{64,0},{128,64},{192,128},{65,1},{129,65},{193,129},{66,2},{130,66... | collective-permute-start | bytes 1572872 | tf_op jit(solution)/shard_map/ppermute | solution.py:44
  727.8 9.9 %copy-start.16 = (f32[384,2048]{1,0:T(8,128)S(1)}, f32[384,2048]{1,0:T(8,128)}, u32[]{:S(2)}) copy-start(f32[384,2048]{1,0:T(8,128)} %reshape.849) | copy-start | bytes 9437188
  728.4 9.3 %copy-start.9 = (f32[1,1,384,2048]{3,2,1,0:T(8,128)S(1)}, f32[1,1,384,2048]{3,2,1,0:T(8,128)}, u32[]{:S(2)}) copy-start(f32[1,1,384,2048]{3,2,1,0:T(8,128)} %param.50) | copy-start | bytes 9437188
where the time goes:
time: 755 us; the launch traced here: 743 us
  local copies, waits for them, and re-layouts  189 us (25%)
  waiting for transfers between devices  157 us (21%)
  blocking collectives  139 us (18%)
  starting transfers between devices  122 us (16%)
  other arithmetic  89.3 us (12%)
  matrix products  46.1 us (6%)
    unnamed x111, local copies, waits for them, and re-layouts  71.2 us
    all_to_all x3, blocking collectives, route_block(): lax.all_to_all(act_block[None], 'replica', split_axis=1, concat_axis=0, t...  66.6 us
    all_to_all x3, blocking collectives, route_block(): lax.all_to_all(reorder(lax.all_to_all(act_block[None], 'replica', split_a...  59.7 us
    all_to_all x2, waiting for transfers between devices, partner_copy(): lax.all_to_all(for_sending(tuple((jnp.take(member, partner, axis=0) for m...  59.5 us
    ppermute x6, waiting for transfers between devices, passed_along(): return lax.ppermute(shard, axis, pairs)  59.2 us
    unnamed x8, other arithmetic  55.5 us
    ppermute x6, starting transfers between devices, passed_along(): return lax.ppermute(shard, axis, pairs)  31.4 us
    all_to_all x3, starting transfers between devices, route_block(): lax.all_to_all(act_block[None], 'replica', split_axis=1, concat_axis=0, t...  28.7 us
  transfers between devices with their start and end apart: 16, of which 11 were waited for; matrix products, arithmetic and copies ran while one was open for 22% of the time, Pallas kernels for 0%

commit v1 on v0

v1 whole, which is shorter than its diff:
```python
import functools

import jax
import jax.numpy as jnp
from jax import lax
from jax.experimental import pallas as pl
from jax.experimental.pallas import tpu as pltpu
from jax.sharding import PartitionSpec as P

EPSILON = 1e-05
OUTER_RATE = 0.7
MOMENTUM = 0.9

MESH = pl.DeviceIdType.MESH
F32 = jnp.float32
BF16 = jnp.bfloat16

NN = (((1,), (0,)), ((), ()))
NT = (((1,), (1,)), ((), ()))
TN = (((0,), (0,)), ((), ()))


def dot(a, b, dims):
    return lax.dot_general(a, b, dims, preferred_element_type=F32)


def kernel(
    sections,
    replicas,
    stride,
    source_ref,
    tokens_ref,
    gate_ref,
    up_ref,
    slow_ref,
    prev_ref,
    new_slow_ref,
    new_outer_ref,
    gate_w,
    up_w,
    slow_w,
    pair_w,
    act,
    out,
    upstream,
    grad,
    spread_in_0,
    spread_in_1,
    spread_out_0,
    spread_out_1,
    gossip_in_0,
    gossip_in_1,
    gossip_out_0,
    gossip_out_1,
    mate,
    velocity,
    inv_rms,
    gate_act,
    up_act,
    hidden,
    load_sem,
    store_sem,
    token_send,
    token_recv,
    first_send,
    first_recv,
    second_send,
    second_recv,
    gossip_send,
    gossip_recv,
):
    spread_in = (spread_in_0, spread_in_1)
    spread_out = (spread_out_0, spread_out_1)
    gossip_in = (gossip_in_0, gossip_in_1)
    gossip_out = (gossip_out_0, gossip_out_1)
    section = lax.axis_index("section")
    replica = lax.axis_index("replica")
    rows, features = act.shape
    units = pair_w.shape[1]
    across = features // spread_in_0.shape[2]
    down = replicas // across

    def load(ref, target, index):
        return pltpu.make_async_copy(ref, target, load_sem.at[index])

    loads = (
        load(slow_ref, slow_w, 0),
        load(prev_ref, pair_w.at[1], 1),
        load(gate_ref, gate_w, 2),
        load(up_ref, up_w, 3),
    )
    for copy in loads:
        copy.start()

    barrier = pltpu.get_barrier_semaphore()

    def greet(target):
        def one(step, carry):
            pl.semaphore_signal(
                barrier,
                inc=1,
                device_id=(target, lax.rem(replica + step, replicas)),
                device_id_type=MESH,
            )
            return carry

        lax.fori_loop(0, replicas, one, 0)

    for target in range(sections):

        @pl.when(section != target)
        def _():
            greet(target)

    def greet_own(step, carry):
        pl.semaphore_signal(
            barrier,
            inc=1,
            device_id=(section, lax.rem(replica + step, replicas)),
            device_id_type=MESH,
        )
        return carry

    lax.fori_loop(1, replicas, greet_own, 0)
    pl.semaphore_wait(barrier, sections * replicas - 1)

    band = rows // sections

    def token_copy(origin):
        return pltpu.make_async_remote_copy(
            src_ref=tokens_ref,
            dst_ref=act.at[pl.ds(pl.multiple_of(origin * band, band), band)],
            send_sem=token_send,
            recv_sem=token_recv,
            device_id=(0, replica),
            device_id_type=MESH,
        )

    @pl.when(section != 0)
    def _():
        token_copy(section).start()

    @pl.when(section == 0)
    def _():
        pltpu.make_async_copy(tokens_ref, act.at[pl.ds(0, band)], token_recv).start()

    def area(ref, index):
        tall, wide = ref.shape[0] // down, ref.shape[1] // across
        top = pl.multiple_of(lax.div(index, across) * tall, tall)
        left = pl.multiple_of(lax.rem(index, across) * wide, wide)
        return ref.at[pl.ds(top, tall), pl.ds(left, wide)]

    def other(step):
        return lax.rem(replica + step * stride, replicas)

    def spread(ref, target, way):
        def one(step, carry):
            peer = other(step)
            pltpu.make_async_remote_copy(
                src_ref=area(ref, peer),
                dst_ref=spread_in[way].at[replica],
                send_sem=first_send.at[way],
                recv_sem=first_recv.at[way],
                device_id=(target, peer),
                device_id_type=MESH,
            ).start()
            return carry

        lax.fori_loop(0, replicas, one, 0)

    def spread_done(ref, way):
        pltpu.make_async_copy(ref, ref, first_send.at[way]).wait()

    def gather(ref, table, way):
        pltpu.make_async_copy(
            spread_in[way], spread_in[way], first_recv.at[way]
        ).wait()

        def pick(step, carry):
            spread_out[way][step] = spread_in[way][source_ref[table, step]]
            return carry

        lax.fori_loop(0, replicas, pick, 0, unroll=8)
        pltpu.make_async_copy(
            spread_out[way].at[replica], area(ref, replica), second_recv.at[way]
        ).start()

        def one(step, carry):
            peer = other(step)
            pltpu.make_async_remote_copy(
                src_ref=spread_out[way].at[peer],
                dst_ref=area(ref, replica),
                send_sem=second_send.at[way],
                recv_sem=second_recv.at[way],
                device_id=(section, peer),
                device_id_type=MESH,
            ).start()
            return carry

        lax.fori_loop(1, replicas, one, 0)
        pltpu.make_async_copy(ref, ref, second_recv.at[way]).wait()

    def gather_done(way):
        part = spread_out[way].at[pl.ds(0, replicas - 1)]
        pltpu.make_async_copy(part, part, second_send.at[way]).wait()

    def gossip_first(part):
        pltpu.make_async_copy(
            area(pair_w.at[part], replica),
            gossip_in[part].at[replica],
            gossip_recv.at[part],
        ).start()

        def one(step, carry):
            peer = other(step)
            pltpu.make_async_remote_copy(
                src_ref=area(pair_w.at[part], peer),
                dst_ref=gossip_in[part].at[replica],
                send_sem=gossip_send.at[part],
                recv_sem=gossip_recv.at[part],
                device_id=(section, peer),
                device_id_type=MESH,
            ).start()
            return carry

        lax.fori_loop(1, replicas, one, 0)

    def gossip_second(part):
        pltpu.make_async_copy(
            gossip_in[part], gossip_in[part], gossip_recv.at[part]
        ).wait()

        def pick(step, carry):
            gossip_out[part][step] = gossip_in[part][source_ref[2 * sections - 2, step]]
            return carry

        lax.fori_loop(0, replicas, pick, 0, unroll=4)
        pltpu.make_async_copy(
            gossip_out[part].at[replica],
            area(mate.at[part], replica),
            gossip_recv.at[2 + part],
        ).start()

        def one(step, carry):
            peer = other(step)
            pltpu.make_async_remote_copy(
                src_ref=gossip_out[part].at[peer],
                dst_ref=area(mate.at[part], replica),
                send_sem=gossip_send.at[2 + part],
                recv_sem=gossip_recv.at[2 + part],
                device_id=(section, peer),
                device_id_type=MESH,
            ).start()
            return carry

        lax.fori_loop(1, replicas, one, 0)

    def gossip_done(part):
        for stage in range(2):
            piece = gossip_out[part].at[pl.ds(0, replicas - 1)]
            pltpu.make_async_copy(piece, piece, gossip_send.at[2 * stage + part]).wait()

    loads[0].wait()
    pair_w[0] = slow_w[...].astype(BF16)
    loads[1].wait()

    @pl.when(section >= sections // 2)
    def _():
        gossip_first(0)

    loads[2].wait()
    loads[3].wait()

    @pl.when(section == 0)
    def _():
        pltpu.make_async_copy(act, act, token_recv).wait()

    @pl.when(section > 0)
    def _():
        gather(act, section - 1, 0)

    wide = act[...].astype(F32)
    scale = lax.rsqrt(jnp.mean(wide * wide, axis=-1, keepdims=True) + EPSILON)
    inv_rms[...] = scale
    normed = (wide * scale).astype(BF16)
    gate = dot(normed, gate_w[...], NN)
    up = dot(normed, up_w[...], NN)
    gate_act[...] = gate
    up_act[...] = up
    hid = (jax.nn.silu(gate) * up).astype(BF16)
    hidden[...] = hid
    result = (act[...].astype(F32) + dot(hid, pair_w[0], NN)).astype(BF16)
    out[...] = result

    @pl.when(section < sections - 1)
    def _():
        spread(out, section + 1, 0)

    @pl.when(section == sections - 1)
    def _():
        upstream[...] = (out[...].astype(F32) / float(rows)).astype(BF16)

    @pl.when(section < sections // 2)
    def _():
        gossip_first(0)
        gossip_first(1)

    @pl.when(section < sections - 1)
    def _():
        gather(upstream, sections - 1 + section, 1)

    above = upstream[...]
    hidden_grad = dot(above, pair_w[0], NT)
    gate = gate_act[...]
    sig = jax.nn.sigmoid(gate)
    gate_grad = (hidden_grad * up_act[...] * sig * (1.0 + gate * (1.0 - sig))).astype(BF16)
    up_grad = (hidden_grad * gate * sig).astype(BF16)

    @pl.when(section > 0)
    def _():
        normed_grad = dot(gate_grad, gate_w[...], NT) + dot(up_grad, up_w[...], NT)
        scale = inv_rms[...]
        wide = act[...].astype(F32)
        mean = jnp.mean(normed_grad * wide, axis=-1, keepdims=True)
        grad[...] = (
            upstream[...].astype(F32) + scale * normed_grad - wide * scale**3 * mean
        ).astype(BF16)
        spread(grad, section - 1, 1)

    @pl.when(section >= sections // 2)
    def _():
        gossip_first(1)

    weight_grad = dot(hidden[...], upstream[...], TN)
    old = pair_w[1].astype(F32)
    speed = (0.5 * MOMENTUM) * old + weight_grad
    velocity[...] = speed
    slow_w[...] = 0.5 * slow_w[...] - OUTER_RATE * (weight_grad + MOMENTUM * speed)

    gossip_second(0)
    gossip_second(1)

    @pl.when(section != 0)
    def _():
        pltpu.make_async_copy(tokens_ref, tokens_ref, token_send).wait()
        gather_done(0)
        spread_done(grad, 1)

    @pl.when(section < sections - 1)
    def _():
        spread_done(out, 0)
        gather_done(1)

    pltpu.make_async_copy(mate.at[0], mate.at[0], gossip_recv.at[2]).wait()
    pltpu.make_async_copy(mate.at[1], mate.at[1], gossip_recv.at[3]).wait()
    for part in range(2):
        gossip_done(part)
    theirs = (0.5 * MOMENTUM) * mate[1].astype(F32)
    slow_w[...] = slow_w[...] + (
        0.5 * mate[0].astype(F32) - (OUTER_RATE * MOMENTUM) * theirs
    )
    gossip = (velocity[...] + theirs).astype(BF16)
    pair_w[0] = gossip
    stores = (
        pltpu.make_async_copy(slow_w, new_slow_ref, store_sem.at[0]),
        pltpu.make_async_copy(pair_w.at[0], new_outer_ref, store_sem.at[1]),
    )
    for copy in stores:
        copy.start()
    for copy in stores:
        copy.wait()


def local(sections, replicas, tokens, gate_weight, up_weight, slow_down, prev_outer, route, partner):
    rows = tokens.shape[1] * sections
    features = tokens.shape[2]
    units = gate_weight.shape[3]
    order = jnp.arange(replicas, dtype=jnp.int32)
    targets = route[:, 0]
    origins = jnp.sum(
        jnp.where(targets[:, :, None] == order, order[:, None], 0), axis=1, dtype=jnp.int32
    )
    sources = jnp.concatenate([origins, targets, partner[None]], axis=0)
    across = min(16, replicas)
    down = replicas // across
    piece = (rows // down, features // across)
    share = (units // down, features // across)
    stride = 37 if replicas == 64 else 1
    anywhere = pl.BlockSpec(memory_space=pl.ANY)
    dma = pltpu.SemaphoreType.DMA
    new_slow, new_outer = pl.pallas_call(
        functools.partial(kernel, sections, replicas, stride),
        out_shape=(
            jax.ShapeDtypeStruct((units, features), F32),
            jax.ShapeDtypeStruct((units, features), BF16),
        ),
        in_specs=[pl.BlockSpec(memory_space=pltpu.SMEM)] + [anywhere] * 5,
        out_specs=(anywhere, anywhere),
        scratch_shapes=[
            pltpu.VMEM((features, units), BF16),
            pltpu.VMEM((features, units), BF16),
            pltpu.VMEM((units, features), F32),
            pltpu.VMEM((2, units, features), BF16),
            pltpu.VMEM((rows, features), BF16),
            pltpu.VMEM((rows, features), BF16),
            pltpu.VMEM((rows, features), BF16),
            pltpu.VMEM((rows, features), BF16),
            pltpu.VMEM((replicas, *piece), BF16),
            pltpu.VMEM((replicas, *piece), BF16),
            pltpu.VMEM((replicas, *piece), BF16),
            pltpu.VMEM((replicas, *piece), BF16),
            pltpu.VMEM((replicas, *share), BF16),
            pltpu.VMEM((replicas, *share), BF16),
            pltpu.VMEM((replicas, *share), BF16),
            pltpu.VMEM((replicas, *share), BF16),
            pltpu.VMEM((2, units, features), BF16),
            pltpu.VMEM((units, features), F32),
            pltpu.VMEM((rows, 1), F32),
            pltpu.VMEM((rows, units), F32),
            pltpu.VMEM((rows, units), F32),
            pltpu.VMEM((rows, units), BF16),
            dma((4,)),
            dma((2,)),
            dma,
            dma,
            dma((2,)),
            dma((2,)),
            dma((2,)),
            dma((2,)),
            dma((4,)),
            dma((4,)),
        ],
        compiler_params=pltpu.CompilerParams(
            collective_id=0, has_side_effects=True, vmem_limit_bytes=60 * 2**20
        ),
        name="relay",
    )(sources, tokens[0], gate_weight[0, 0], up_weight[0, 0], slow_down[0, 0], prev_outer[0, 0])
    return (new_slow[None, None], new_outer[None, None])


def solution(mesh):
    sections, replicas = mesh.shape["section"], mesh.shape["replica"]
    own = P("section", "replica", None, None)
    return jax.shard_map(
        functools.partial(local, sections, replicas),
        mesh=mesh,
        in_specs=(P("replica", "section", None), own, own, own, own, P(), P()),
        out_specs=(own, own),
        check_vma=False,
    )
```

time: 755 us -> 262 us (0.35)
  the two profiles are of different devices: /device:TPU:1 before, /device:TPU:8 now
where the time goes in v1:
time: 262 us
  Pallas kernels  254 us (97%)
  local copies, waits for them, and re-layouts  5.85 us (2%)
    pallas_call x1, Pallas kernels, local(): pl.pallas_call(functools.partial(kernel, sections, replicas, stride), out...  254 us
    unnamed x5, local copies, waits for them, and re-layouts  5.85 us

profile of v1, /device:TPU:8, one launch (start us, length us, event | category | flops | bytes accessed | tf_op | source)
XLA Modules:
  0.0 261.8 jit_solution(16695611708681028630)
XLA Ops:
  0.6 0.7 copy.11
  1.3 0.1 select_reduce_fusion
  1.4 1.3 pad_add_fusion.source_ref
  2.7 254.0 %relay.1 = (f32[384,2048]{1,0:T(8,128)}, bf16[384,2048]{1,0:T(8,128)(2,1)}) custom-call(s32[7,64]{1,0:T(8,128)} %pad_add_fusion.source_ref, bf16[32,2048]{1,0:T(8,128)(2,1)} %bitcast.17, bf16[2048,384]{1,0:T(8,128)(2,1)} %bitcast.13, bf16[2048,384]{1,0:T(8,128)(2,1)} %bitcast.14, f32[384,2048]{1,0:T(8,128)} %bitcast.11, bf16[384,2048]{1,0:T(8,128)(2,1)} %bitcast.15), custom_call_target="tpu_custom_call" | custom-call | tf_op jit(solution)/shard_map/relay/pallas_call | solution.py:391
  256.6 0.0 copy-start
  256.7 4.0 %copy.14 = f32[1,1,384,2048]{3,2,1,0:T(8,128)} copy(f32[1,1,384,2048]{3,2,1,0:T(8,128)} %bitcast.12) | data formatting | bytes 6291456
  260.7 0.0 copy-done
  260.7 1.1 copy.15
Async XLA Ops:
  256.6 4.0 %copy-start = (bf16[384,2048]{1,0:T(8,128)(2,1)S(1)}, bf16[384,2048]{1,0:T(8,128)(2,1)}, u32[]{:S(2)}) copy-start(bf16[384,2048]{1,0:T(8,128)(2,1)} %get-tuple-element.5) | copy-start | bytes 4718596

commit v2 on v1

--- a/solution.py
+++ b/solution.py
@@ -28,14 +28,17 @@
     sections,
     replicas,
     stride,
+    torus,
     source_ref,
     tokens_ref,
     gate_ref,
     up_ref,
     slow_ref,
     prev_ref,
-    new_slow_ref,
-    new_outer_ref,
+    slow_out,
+    velocity_out,
+    mate_slow,
+    mate_prev,
     gate_w,
     up_w,
     slow_w,
@@ -52,7 +55,6 @@
     gossip_in_1,
     gossip_out_0,
     gossip_out_1,
-    mate,
     velocity,
     inv_rms,
     gate_act,
@@ -69,6 +71,7 @@
     gossip_send,
     gossip_recv,
 ):
+    mate = (mate_slow, mate_prev)
     spread_in = (spread_in_0, spread_in_1)
     spread_out = (spread_out_0, spread_out_1)
     gossip_in = (gossip_in_0, gossip_in_1)
@@ -153,9 +156,20 @@
     def other(step):
         return lax.rem(replica + step * stride, replicas)
 
+    def turn(position, index, length):
+        ahead = lax.div(index + 1, 2) * (1 - 2 * lax.rem(index, 2))
+        return lax.rem(position + length // 2 + ahead, length)
+
+    def far_first(step):
+        width, depth, height = torus
+        x = turn(lax.div(replica, depth * height), lax.rem(lax.div(step, height), width), width)
+        z = turn(lax.rem(lax.div(replica, height), depth), lax.div(step, height * width), depth)
+        y = turn(lax.rem(replica, height), lax.rem(step, height), height)
+        return (x * depth + z) * height + y
+
     def spread(ref, target, way):
         def one(step, carry):
-            peer = other(step)
+            peer = far_first(step)
             pltpu.make_async_remote_copy(
                 src_ref=area(ref, peer),
                 dst_ref=spread_in[way].at[replica],
@@ -186,7 +200,7 @@
         ).start()
 
         def one(step, carry):
-            peer = other(step)
+            peer = far_first(step)
             pltpu.make_async_remote_copy(
                 src_ref=spread_out[way].at[peer],
                 dst_ref=area(ref, replica),
@@ -197,7 +211,7 @@
             ).start()
             return carry
 
-        lax.fori_loop(1, replicas, one, 0)
+        lax.fori_loop(0, replicas - 1, one, 0)
         pltpu.make_async_copy(ref, ref, second_recv.at[way]).wait()
 
     def gather_done(way):
@@ -237,7 +251,7 @@
         lax.fori_loop(0, replicas, pick, 0, unroll=4)
         pltpu.make_async_copy(
             gossip_out[part].at[replica],
-            area(mate.at[part], replica),
+            area(mate[part], replica),
             gossip_recv.at[2 + part],
         ).start()
 
@@ -245,7 +259,7 @@
             peer = other(step)
             pltpu.make_async_remote_copy(
                 src_ref=gossip_out[part].at[peer],
-                dst_ref=area(mate.at[part], replica),
+                dst_ref=area(mate[part], replica),
                 send_sem=gossip_send.at[2 + part],
                 recv_sem=gossip_recv.at[2 + part],
                 device_id=(section, peer),
@@ -267,6 +281,7 @@
     @pl.when(section >= sections // 2)
     def _():
         gossip_first(0)
+        gossip_first(1)
 
     loads[2].wait()
     loads[3].wait()
@@ -304,20 +319,19 @@
     def _():
         gossip_first(0)
         gossip_first(1)
+        gossip_second(0)
 
     @pl.when(section < sections - 1)
     def _():
         gather(upstream, sections - 1 + section, 1)
 
-    above = upstream[...]
-    hidden_grad = dot(above, pair_w[0], NT)
-    gate = gate_act[...]
-    sig = jax.nn.sigmoid(gate)
-    gate_grad = (hidden_grad * up_act[...] * sig * (1.0 + gate * (1.0 - sig))).astype(BF16)
-    up_grad = (hidden_grad * gate * sig).astype(BF16)
-
     @pl.when(section > 0)
     def _():
+        hidden_grad = dot(upstream[...], pair_w[0], NT)
+        gate = gate_act[...]
+        sig = jax.nn.sigmoid(gate)
+        gate_grad = (hidden_grad * up_act[...] * sig * (1.0 + gate * (1.0 - sig))).astype(BF16)
+        up_grad = (hidden_grad * gate * sig).astype(BF16)
         normed_grad = dot(gate_grad, gate_w[...], NT) + dot(up_grad, up_w[...], NT)
         scale = inv_rms[...]
         wide = act[...].astype(F32)
@@ -329,16 +343,20 @@
 
     @pl.when(section >= sections // 2)
     def _():
-        gossip_first(1)
+        gossip_second(0)
+
+    gossip_second(1)
 
     weight_grad = dot(hidden[...], upstream[...], TN)
-    old = pair_w[1].astype(F32)
-    speed = (0.5 * MOMENTUM) * old + weight_grad
+    speed = (0.5 * MOMENTUM) * pair_w[1].astype(F32) + weight_grad
     velocity[...] = speed
     slow_w[...] = 0.5 * slow_w[...] - OUTER_RATE * (weight_grad + MOMENTUM * speed)
-
-    gossip_second(0)
-    gossip_second(1)
+    stores = (
+        pltpu.make_async_copy(slow_w, slow_out, store_sem.at[0]),
+        pltpu.make_async_copy(velocity, velocity_out, store_sem.at[1]),
+    )
+    for copy in stores:
+        copy.start()
 
     @pl.when(section != 0)
     def _():
@@ -351,22 +369,9 @@
         spread_done(out, 0)
         gather_done(1)
 
-    pltpu.make_async_copy(mate.at[0], mate.at[0], gossip_recv.at[2]).wait()
-    pltpu.make_async_copy(mate.at[1], mate.at[1], gossip_recv.at[3]).wait()
     for part in range(2):
+        pltpu.make_async_copy(mate[part], mate[part], gossip_recv.at[2 + part]).wait()
         gossip_done(part)
-    theirs = (0.5 * MOMENTUM) * mate[1].astype(F32)
-    slow_w[...] = slow_w[...] + (
-        0.5 * mate[0].astype(F32) - (OUTER_RATE * MOMENTUM) * theirs
-    )
-    gossip = (velocity[...] + theirs).astype(BF16)
-    pair_w[0] = gossip
-    stores = (
-        pltpu.make_async_copy(slow_w, new_slow_ref, store_sem.at[0]),
-        pltpu.make_async_copy(pair_w.at[0], new_outer_ref, store_sem.at[1]),
-    )
-    for copy in stores:
-        copy.start()
     for copy in stores:
         copy.wait()
 
@@ -386,16 +391,19 @@
     piece = (rows // down, features // across)
     share = (units // down, features // across)
     stride = 37 if replicas == 64 else 1
+    torus = (4, 8, 2) if replicas == 64 else (1, replicas, 1)
     anywhere = pl.BlockSpec(memory_space=pl.ANY)
     dma = pltpu.SemaphoreType.DMA
-    new_slow, new_outer = pl.pallas_call(
-        functools.partial(kernel, sections, replicas, stride),
+    slow, velocity, mate_slow, mate_prev = pl.pallas_call(
+        functools.partial(kernel, sections, replicas, stride, torus),
         out_shape=(
             jax.ShapeDtypeStruct((units, features), F32),
+            jax.ShapeDtypeStruct((units, features), F32),
+            jax.ShapeDtypeStruct((units, features), BF16),
             jax.ShapeDtypeStruct((units, features), BF16),
         ),
         in_specs=[pl.BlockSpec(memory_space=pltpu.SMEM)] + [anywhere] * 5,
-        out_specs=(anywhere, anywhere),
+        out_specs=(anywhere,) * 4,
         scratch_shapes=[
             pltpu.VMEM((features, units), BF16),
             pltpu.VMEM((features, units), BF16),
@@ -413,7 +421,6 @@
             pltpu.VMEM((replicas, *share), BF16),
             pltpu.VMEM((replicas, *share), BF16),
             pltpu.VMEM((replicas, *share), BF16),
-            pltpu.VMEM((2, units, features), BF16),
             pltpu.VMEM((units, features), F32),
             pltpu.VMEM((rows, 1), F32),
             pltpu.VMEM((rows, units), F32),
@@ -435,6 +442,9 @@
         ),
         name="relay",
     )(sources, tokens[0], gate_weight[0, 0], up_weight[0, 0], slow_down[0, 0], prev_outer[0, 0])
+    theirs = (0.5 * MOMENTUM) * mate_prev.astype(F32)
+    new_slow = slow + (0.5 * mate_slow.astype(F32) - (OUTER_RATE * MOMENTUM) * theirs)
+    new_outer = (velocity + theirs).astype(BF16)
     return (new_slow[None, None], new_outer[None, None])
 
 

time: 262 us -> 229 us (0.87)
  Pallas kernels: 254 us -> 219 us
  other arithmetic: 1.37 us -> 8.58 us
  local copies, waits for them, and re-layouts: 5.85 us -> 0.68 us
    pallas_call x1, Pallas kernels: 254 us -> 219 us  [local(): pl.pallas_call(functools.partial(kernel, sections, replicas, stride, toru...]
    broadcast_in_dim x0 -> x1, other arithmetic: none -> 7.22 us  [local(): return (new_slow[None, None], new_outer[None, None])]
    unnamed x5 -> x1, local copies, waits for them, and re-layouts: 5.85 us -> 0.68 us
where the time goes in v2:
time: 229 us
  Pallas kernels  219 us (96%)
  other arithmetic  8.58 us (4%)
    pallas_call x1, Pallas kernels, local(): pl.pallas_call(functools.partial(kernel, sections, replicas, stride, toru...  219 us
    broadcast_in_dim x1, other arithmetic, local(): return (new_slow[None, None], new_outer[None, None])  7.22 us

profile of v2, /device:TPU:8, one launch (start us, length us, event | category | flops | bytes accessed | tf_op | source)
XLA Modules:
  0.0 228.8 jit_solution(14729384601577383553)
XLA Ops:
  0.6 0.7 copy.11
  1.3 0.1 select_reduce_fusion
  1.4 1.3 pad_add_fusion.source_ref
  2.7 218.9 %relay.1 = (f32[384,2048]{1,0:T(8,128)}, f32[384,2048]{1,0:T(8,128)}, bf16[384,2048]{1,0:T(8,128)(2,1)}, bf16[384,2048]{1,0:T(8,128)(2,1)}) custom-call(s32[7,64]{1,0:T(8,128)} %pad_add_fusion.source_ref, bf16[32,2048]{1,0:T(8,128)(2,1)} %bitcast.17, bf16[2048,384]{1,0:T(8,128)(2,1)} %bitcast.14, bf16[2048,384]{1,0:T(8,128)(2,1)} %bitcast.15, ...), custom_call_target="tpu_custom_call" | custom-call | tf_op jit(solution)/shard_map/relay/pallas_call | solution.py:397
  221.6 7.2 %fusion.5 = (bf16[1,1,384,2048]{3,2,1,0:T(8,128)(2,1)}, f32[1,1,384,2048]{3,2,1,0:T(8,128)}) fusion(f32[384,2048]{1,0:T(8,128)} %get-tuple-element.9, bf16[384,2048]{1,0:T(8,128)(2,1)} %get-tuple-element.8, f32[384,2048]{1,0:T(8,128)} %get-tuple-element.6, bf16[384,2048]{1,0:T(8,128)(2,1)} %get-tuple-element.7), kind=kLoop, calls=%fused_computation.7 | loop fusion | flops 7077888 | bytes 14155776 | tf_op jit(solution)/shard_map/broadcast_in_dim | solution.py:448

commit v3 on v2

--- a/solution.py
+++ b/solution.py
@@ -29,7 +29,9 @@
     replicas,
     stride,
     torus,
-    source_ref,
+    origin_ref,
+    target_ref,
+    partner_ref,
     tokens_ref,
     gate_ref,
     up_ref,
@@ -53,8 +55,12 @@
     spread_out_1,
     gossip_in_0,
     gossip_in_1,
+    gossip_in_2,
+    gossip_in_3,
     gossip_out_0,
     gossip_out_1,
+    gossip_out_2,
+    gossip_out_3,
     velocity,
     inv_rms,
     gate_act,
@@ -70,12 +76,15 @@
     second_recv,
     gossip_send,
     gossip_recv,
+    mate_send,
+    mate_recv,
+    gate_sem,
 ):
     mate = (mate_slow, mate_prev)
     spread_in = (spread_in_0, spread_in_1)
     spread_out = (spread_out_0, spread_out_1)
-    gossip_in = (gossip_in_0, gossip_in_1)
-    gossip_out = (gossip_out_0, gossip_out_1)
+    gossip_in = (gossip_in_0, gossip_in_1, gossip_in_2, gossip_in_3)
+    gossip_out = (gossip_out_0, gossip_out_1, gossip_out_2, gossip_out_3)
     section = lax.axis_index("section")
     replica = lax.axis_index("replica")
     rows, features = act.shape
@@ -185,13 +194,13 @@
     def spread_done(ref, way):
         pltpu.make_async_copy(ref, ref, first_send.at[way]).wait()
 
-    def gather(ref, table, way):
+    def gather(ref, table, row, way):
         pltpu.make_async_copy(
             spread_in[way], spread_in[way], first_recv.at[way]
         ).wait()
 
         def pick(step, carry):
-            spread_out[way][step] = spread_in[way][source_ref[table, step]]
+            spread_out[way][step] = spread_in[way][table[row, step]]
             return carry
 
         lax.fori_loop(0, replicas, pick, 0, unroll=8)
@@ -218,61 +227,89 @@
         part = spread_out[way].at[pl.ds(0, replicas - 1)]
         pltpu.make_async_copy(part, part, second_send.at[way]).wait()
 
+    half = lax.div(section, 2)
+    helper = half * (sections - 1)
+    helping = section == helper
+
     def gossip_first(part):
-        pltpu.make_async_copy(
-            area(pair_w.at[part], replica),
-            gossip_in[part].at[replica],
-            gossip_recv.at[part],
-        ).start()
+        for origin in range(2):
+            landing = gossip_in[2 * origin + part]
+
+            @pl.when(lax.rem(section, 2) == origin)
+            def _():
+                @pl.when(helping)
+                def _():
+                    pltpu.make_async_copy(
+                        area(pair_w.at[part], replica),
+                        landing.at[replica],
+                        gossip_recv.at[2 * origin + part],
+                    ).start()
+
+                def one(step, carry):
+                    peer = other(step)
+                    pltpu.make_async_remote_copy(
+                        src_ref=area(pair_w.at[part], peer),
+                        dst_ref=landing.at[replica],
+                        send_sem=gossip_send.at[part],
+                        recv_sem=gossip_recv.at[2 * origin + part],
+                        device_id=(helper, peer),
+                        device_id_type=MESH,
+                    ).start()
+                    return carry
+
+                lax.fori_loop(jnp.where(helping, 1, 0), replicas, one, 0)
+
+    def gossip_second(origin, part):
+        arrived, leaving = gossip_in[2 * origin + part], gossip_out[2 * origin + part]
+        target = 2 * half + origin
+        pltpu.make_async_copy(arrived, arrived, gossip_recv.at[2 * origin + part]).wait()
+
+        def pick(step, carry):
+            leaving[step] = arrived[partner_ref[step]]
+            return carry
+
+        lax.fori_loop(0, replicas, pick, 0, unroll=4)
+
+        @pl.when(target == section)
+        def _():
+            pltpu.make_async_copy(
+                leaving.at[replica], area(mate[part], replica), mate_recv.at[part]
+            ).start()
 
         def one(step, carry):
             peer = other(step)
             pltpu.make_async_remote_copy(
-                src_ref=area(pair_w.at[part], peer),
-                dst_ref=gossip_in[part].at[replica],
-                send_sem=gossip_send.at[part],
-                recv_sem=gossip_recv.at[part],
-                device_id=(section, peer),
+                src_ref=leaving.at[peer],
+                dst_ref=area(mate[part], replica),
+                send_sem=mate_send.at[2 * origin + part],
+                recv_sem=mate_recv.at[part],
+                device_id=(target, peer),
                 device_id_type=MESH,
             ).start()
             return carry
 
-        lax.fori_loop(1, replicas, one, 0)
-
-    def gossip_second(part):
-        pltpu.make_async_copy(
-            gossip_in[part], gossip_in[part], gossip_recv.at[part]
-        ).wait()
-
-        def pick(step, carry):
-            gossip_out[part][step] = gossip_in[part][source_ref[2 * sections - 2, step]]
-            return carry
-
-        lax.fori_loop(0, replicas, pick, 0, unroll=4)
-        pltpu.make_async_copy(
-            gossip_out[part].at[replica],
-            area(mate[part], replica),
-            gossip_recv.at[2 + part],
-        ).start()
-
-        def one(step, carry):
-            peer = other(step)
-            pltpu.make_async_remote_copy(
-                src_ref=gossip_out[part].at[peer],
-                dst_ref=area(mate[part], replica),
-                send_sem=gossip_send.at[2 + part],
-                recv_sem=gossip_recv.at[2 + part],
-                device_id=(section, peer),
-                device_id_type=MESH,
-            ).start()
-            return carry
-
-        lax.fori_loop(1, replicas, one, 0)
-
-    def gossip_done(part):
-        for stage in range(2):
-            piece = gossip_out[part].at[pl.ds(0, replicas - 1)]
-            pltpu.make_async_copy(piece, piece, gossip_send.at[2 * stage + part]).wait()
+        lax.fori_loop(jnp.where(target == section, 1, 0), replicas, one, 0)
+
+    def sent(sem, alone):
+        whole, most = gossip_out[0], gossip_out[0].at[pl.ds(0, replicas - 1)]
+
+        @pl.when(alone)
+        def _():
+            pltpu.make_async_copy(most, most, sem).wait()
+
+        @pl.when(jnp.logical_not(alone))
+        def _():
+            pltpu.make_async_copy(whole, whole, sem).wait()
+
+    def gossip_done():
+        for part in range(2):
+            sent(gossip_send.at[part], helping)
+
+        @pl.when(helping)
+        def _():
+            for origin in range(2):
+                for part in range(2):
+                    sent(mate_send.at[2 * origin + part], 2 * half + origin == section)
 
     loads[0].wait()
     pair_w[0] = slow_w[...].astype(BF16)
@@ -281,6 +318,9 @@
     @pl.when(section >= sections // 2)
     def _():
         gossip_first(0)
+
+    @pl.when(section == sections - 1)
+    def _():
         gossip_first(1)
 
     loads[2].wait()
@@ -292,7 +332,7 @@
 
     @pl.when(section > 0)
     def _():
-        gather(act, section - 1, 0)
+        gather(act, origin_ref, section - 1, 0)
 
     wide = act[...].astype(F32)
     scale = lax.rsqrt(jnp.mean(wide * wide, axis=-1, keepdims=True) + EPSILON)
@@ -315,15 +355,28 @@
     def _():
         upstream[...] = (out[...].astype(F32) / float(rows)).astype(BF16)
 
-    @pl.when(section < sections // 2)
-    def _():
+    @pl.when(section == 1)
+    def _():
+        spread_done(out, 0)
+        pl.semaphore_signal(gate_sem, inc=1, device_id=(0, replica), device_id_type=MESH)
         gossip_first(0)
+
+    @pl.when((section > 0) & (section < sections - 1))
+    def _():
         gossip_first(1)
-        gossip_second(0)
+
+    @pl.when(section == 0)
+    def _():
+        gossip_first(0)
+        pl.semaphore_wait(gate_sem, 1)
+        gossip_first(1)
+        for part in range(2):
+            for origin in range(2):
+                gossip_second(origin, part)
 
     @pl.when(section < sections - 1)
     def _():
-        gather(upstream, sections - 1 + section, 1)
+        gather(upstream, target_ref, section, 1)
 
     @pl.when(section > 0)
     def _():
@@ -341,11 +394,11 @@
         ).astype(BF16)
         spread(grad, section - 1, 1)
 
-    @pl.when(section >= sections // 2)
-    def _():
-        gossip_second(0)
-
-    gossip_second(1)
+    @pl.when(section == sections - 1)
+    def _():
+        for part in range(2):
+            for origin in range(2):
+                gossip_second(origin, part)
 
     weight_grad = dot(hidden[...], upstream[...], TN)
     speed = (0.5 * MOMENTUM) * pair_w[1].astype(F32) + weight_grad
@@ -364,14 +417,17 @@
         gather_done(0)
         spread_done(grad, 1)
 
+    @pl.when((section < sections - 1) & (section != 1))
+    def _():
+        spread_done(out, 0)
+
     @pl.when(section < sections - 1)
     def _():
-        spread_done(out, 0)
         gather_done(1)
 
     for part in range(2):
-        pltpu.make_async_copy(mate[part], mate[part], gossip_recv.at[2 + part]).wait()
-        gossip_done(part)
+        pltpu.make_async_copy(mate[part], mate[part], mate_recv.at[part]).wait()
+    gossip_done()
     for copy in stores:
         copy.wait()
 
@@ -385,7 +441,6 @@
     origins = jnp.sum(
         jnp.where(targets[:, :, None] == order, order[:, None], 0), axis=1, dtype=jnp.int32
     )
-    sources = jnp.concatenate([origins, targets, partner[None]], axis=0)
     across = min(16, replicas)
     down = replicas // across
     piece = (rows // down, features // across)
@@ -402,7 +457,7 @@
             jax.ShapeDtypeStruct((units, features), BF16),
             jax.ShapeDtypeStruct((units, features), BF16),
         ),
-        in_specs=[pl.BlockSpec(memory_space=pltpu.SMEM)] + [anywhere] * 5,
+        in_specs=[pl.BlockSpec(memory_space=pltpu.SMEM)] * 3 + [pl.BlockSpec(memory_space=pltpu.HBM)] * 5,
         out_specs=(anywhere,) * 4,
         scratch_shapes=[
             pltpu.VMEM((features, units), BF16),
@@ -421,6 +476,10 @@
             pltpu.VMEM((replicas, *share), BF16),
             pltpu.VMEM((replicas, *share), BF16),
             pltpu.VMEM((replicas, *share), BF16),
+            pltpu.VMEM((replicas, *share), BF16),
+            pltpu.VMEM((replicas, *share), BF16),
+            pltpu.VMEM((replicas, *share), BF16),
+            pltpu.VMEM((replicas, *share), BF16),
             pltpu.VMEM((units, features), F32),
             pltpu.VMEM((rows, 1), F32),
             pltpu.VMEM((rows, units), F32),
@@ -434,14 +493,26 @@
             dma((2,)),
             dma((2,)),
             dma((2,)),
+            dma((2,)),
             dma((4,)),
             dma((4,)),
+            dma((2,)),
+            pltpu.SemaphoreType.REGULAR,
         ],
         compiler_params=pltpu.CompilerParams(
-            collective_id=0, has_side_effects=True, vmem_limit_bytes=60 * 2**20
+            collective_id=0, has_side_effects=True, vmem_limit_bytes=40 * 2**20
         ),
         name="relay",
-    )(sources, tokens[0], gate_weight[0, 0], up_weight[0, 0], slow_down[0, 0], prev_outer[0, 0])
+    )(
+        origins,
+        targets,
+        partner,
+        pltpu.with_memory_space_constraint(tokens[0], pltpu.HBM),
+        pltpu.with_memory_space_constraint(gate_weight[0, 0], pltpu.HBM),
+        pltpu.with_memory_space_constraint(up_weight[0, 0], pltpu.HBM),
+        pltpu.with_memory_space_constraint(slow_down[0, 0], pltpu.HBM),
+        pltpu.with_memory_space_constraint(prev_outer[0, 0], pltpu.HBM),
+    )
     theirs = (0.5 * MOMENTUM) * mate_prev.astype(F32)
     new_slow = slow + (0.5 * mate_slow.astype(F32) - (OUTER_RATE * MOMENTUM) * theirs)
     new_outer = (velocity + theirs).astype(BF16)

time: 229 us -> 208 us (0.908)
  Pallas kernels: 219 us -> 203 us
  other arithmetic: 8.58 us -> 3.39 us
    pallas_call x1, Pallas kernels: 219 us -> 203 us  [local(): pl.pallas_call(functools.partial(kernel, sections, replicas, stride, toru...]
    broadcast_in_dim x1, other arithmetic: 7.22 us -> 3.29 us  [local(): return (new_slow[None, None], new_outer[None, None])]
where the time goes in v3:
time: 208 us
  Pallas kernels  203 us (98%)
  other arithmetic  3.39 us (2%)
    pallas_call x1, Pallas kernels, local(): pl.pallas_call(functools.partial(kernel, sections, replicas, stride, toru...  203 us

profile of v3, /device:TPU:8, one launch (start us, length us, event | category | flops | bytes accessed | tf_op | source)
XLA Modules:
  0.0 208.0 jit_solution(447247878181026142)
XLA Ops:
  0.6 0.7 copy.11
  1.3 0.1 select_reduce_fusion.origin_ref
  1.4 0.0 copy-start
  1.4 0.6 copy-done
  2.1 202.6 %relay.1 = (f32[384,2048]{1,0:T(8,128)S(1)}, f32[384,2048]{1,0:T(8,128)S(1)}, bf16[384,2048]{1,0:T(8,128)(2,1)S(1)}, bf16[384,2048]{1,0:T(8,128)(2,1)S(1)}) custom-call(s32[3,64]{1,0:T(4,128)S(1)} %select_reduce_fusion.origin_ref, s32[3,64]{1,0:T(4,128)S(1)} %bitcast.13, s32[64]{0:T(128)S(1)} %copy-done, bf16[32,2048]{1,0:T(8,128)(2,1)} %bitcast.18, ...), custom_call_target="tpu_custom_call" | custom-call | tf_op jit(solution)/shard_map/relay/pallas_call | solution.py:452
  204.7 3.3 %fusion.5 = (bf16[1,1,384,2048]{3,2,1,0:T(8,128)(2,1)}, f32[1,1,384,2048]{3,2,1,0:T(8,128)}) fusion(f32[384,2048]{1,0:T(8,128)S(1)} %get-tuple-element.9, bf16[384,2048]{1,0:T(8,128)(2,1)S(1)} %get-tuple-element.8, f32[384,2048]{1,0:T(8,128)S(1)} %get-tuple-element.6, bf16[384,2048]{1,0:T(8,128)(2,1)S(1)} %get-tuple-element.7), kind=kLoop, calls=%fused_computation.7 | loop fusion | flops 7077888 | bytes 14155776 | tf_op jit(solution)/shard_map/broadcast_in_dim | solution.py:519
Async XLA Ops:
  1.4 0.7 copy-start

commit v4 on v3

--- a/solution.py
+++ b/solution.py
@@ -171,9 +171,9 @@
 
     def far_first(step):
         width, depth, height = torus
-        x = turn(lax.div(replica, depth * height), lax.rem(lax.div(step, height), width), width)
-        z = turn(lax.rem(lax.div(replica, height), depth), lax.div(step, height * width), depth)
-        y = turn(lax.rem(replica, height), lax.rem(step, height), height)
+        x = turn(lax.div(replica, depth * height), lax.div(step, depth * height), width)
+        z = turn(lax.rem(lax.div(replica, height), depth), lax.rem(step, depth), depth)
+        y = turn(lax.rem(replica, height), lax.rem(lax.div(step, depth), height), height)
         return (x * depth + z) * height + y
 
     def spread(ref, target, way):

time: 208 us -> 207 us (level)
  no operation moved by 1% of the time
where the time goes in v4:
time: 207 us
  Pallas kernels  202 us (98%)
  other arithmetic  3.39 us (2%)
    pallas_call x1, Pallas kernels, local(): pl.pallas_call(functools.partial(kernel, sections, replicas, stride, toru...  202 us

profile of v4, /device:TPU:8, one launch (start us, length us, event | category | flops | bytes accessed | tf_op | source)
XLA Modules:
  0.0 207.3 jit_solution(71478572664263120)
XLA Ops:
  0.6 0.7 copy.11
  1.3 0.1 select_reduce_fusion.origin_ref
  1.4 0.0 copy-start
  1.4 0.6 copy-done
  2.1 202.0 %relay.1 = (f32[384,2048]{1,0:T(8,128)S(1)}, f32[384,2048]{1,0:T(8,128)S(1)}, bf16[384,2048]{1,0:T(8,128)(2,1)S(1)}, bf16[384,2048]{1,0:T(8,128)(2,1)S(1)}) custom-call(s32[3,64]{1,0:T(4,128)S(1)} %select_reduce_fusion.origin_ref, s32[3,64]{1,0:T(4,128)S(1)} %bitcast.13, s32[64]{0:T(128)S(1)} %copy-done, bf16[32,2048]{1,0:T(8,128)(2,1)} %bitcast.18, ...), custom_call_target="tpu_custom_call" | custom-call | tf_op jit(solution)/shard_map/relay/pallas_call | solution.py:452
  204.1 3.3 %fusion.5 = (bf16[1,1,384,2048]{3,2,1,0:T(8,128)(2,1)}, f32[1,1,384,2048]{3,2,1,0:T(8,128)}) fusion(f32[384,2048]{1,0:T(8,128)S(1)} %get-tuple-element.9, bf16[384,2048]{1,0:T(8,128)(2,1)S(1)} %get-tuple-element.8, f32[384,2048]{1,0:T(8,128)S(1)} %get-tuple-element.6, bf16[384,2048]{1,0:T(8,128)(2,1)S(1)} %get-tuple-element.7), kind=kLoop, calls=%fused_computation.7 | loop fusion | flops 7077888 | bytes 14155776 | tf_op jit(solution)/shard_map/broadcast_in_dim | solution.py:519
Async XLA Ops:
  1.4 0.7 copy-start

commit v5 on v4

--- a/solution.py
+++ b/solution.py
@@ -116,7 +116,7 @@
             )
             return carry
 
-        lax.fori_loop(0, replicas, one, 0)
+        lax.fori_loop(0, replicas, one, 0, unroll=4)
 
     for target in range(sections):
 
@@ -400,16 +400,19 @@
             for origin in range(2):
                 gossip_second(origin, part)
 
-    weight_grad = dot(hidden[...], upstream[...], TN)
-    speed = (0.5 * MOMENTUM) * pair_w[1].astype(F32) + weight_grad
-    velocity[...] = speed
-    slow_w[...] = 0.5 * slow_w[...] - OUTER_RATE * (weight_grad + MOMENTUM * speed)
-    stores = (
-        pltpu.make_async_copy(slow_w, slow_out, store_sem.at[0]),
-        pltpu.make_async_copy(velocity, velocity_out, store_sem.at[1]),
-    )
-    for copy in stores:
-        copy.start()
+    stores = []
+    for block in range(units // 128):
+        lines = pl.ds(block * 128, 128)
+        weight_grad = dot(hidden[:, lines], upstream[...], TN)
+        speed = (0.5 * MOMENTUM) * pair_w[1, lines].astype(F32) + weight_grad
+        velocity[lines] = speed
+        slow_w[lines] = 0.5 * slow_w[lines] - OUTER_RATE * (weight_grad + MOMENTUM * speed)
+        for index, (kept, target) in enumerate(((slow_w, slow_out), (velocity, velocity_out))):
+            copy = pltpu.make_async_copy(
+                kept.at[lines], target.at[lines], store_sem.at[index, block]
+            )
+            copy.start()
+            stores.append(copy)
 
     @pl.when(section != 0)
     def _():
@@ -486,7 +489,7 @@
             pltpu.VMEM((rows, units), F32),
             pltpu.VMEM((rows, units), BF16),
             dma((4,)),
-            dma((2,)),
+            dma((2, units // 128)),
             dma,
             dma,
             dma((2,)),

time: 207 us -> 207 us (level)
  no operation moved by 1% of the time
where the time goes in v5:
time: 207 us
  Pallas kernels  202 us (98%)
  other arithmetic  3.39 us (2%)
    pallas_call x1, Pallas kernels, local(): pl.pallas_call(functools.partial(kernel, sections, replicas, stride, toru...  202 us

profile of v5, /device:TPU:8, one launch (start us, length us, event | category | flops | bytes accessed | tf_op | source)
XLA Modules:
  0.0 207.0 jit_solution(2479475217936691252)
XLA Ops:
  0.6 0.7 copy.11
  1.3 0.1 select_reduce_fusion.origin_ref
  1.4 0.0 copy-start
  1.4 0.6 copy-done
  2.1 201.6 %relay.1 = (f32[384,2048]{1,0:T(8,128)S(1)}, f32[384,2048]{1,0:T(8,128)S(1)}, bf16[384,2048]{1,0:T(8,128)(2,1)S(1)}, bf16[384,2048]{1,0:T(8,128)(2,1)S(1)}) custom-call(s32[3,64]{1,0:T(4,128)S(1)} %select_reduce_fusion.origin_ref, s32[3,64]{1,0:T(4,128)S(1)} %bitcast.13, s32[64]{0:T(128)S(1)} %copy-done, bf16[32,2048]{1,0:T(8,128)(2,1)} %bitcast.18, ...), custom_call_target="tpu_custom_call" | custom-call | tf_op jit(solution)/shard_map/relay/pallas_call | solution.py:455
  203.7 3.3 %fusion.5 = (bf16[1,1,384,2048]{3,2,1,0:T(8,128)(2,1)}, f32[1,1,384,2048]{3,2,1,0:T(8,128)}) fusion(f32[384,2048]{1,0:T(8,128)S(1)} %get-tuple-element.9, bf16[384,2048]{1,0:T(8,128)(2,1)S(1)} %get-tuple-element.8, f32[384,2048]{1,0:T(8,128)S(1)} %get-tuple-element.6, bf16[384,2048]{1,0:T(8,128)(2,1)S(1)} %get-tuple-element.7), kind=kLoop, calls=%fused_computation.7 | loop fusion | flops 7077888 | bytes 14155776 | tf_op jit(solution)/shard_map/broadcast_in_dim | solution.py:522
Async XLA Ops:
  1.4 0.7 copy-start
